TPU v7x, 32 devices: a whole 2x2x4 slice. The times are simulated.
32 devices in a mesh: rep: 4 (over z), seq: 8 (over y, x, core).
Axes of the slice: x: 2, y: 2, z: 4, core: 2. Of those that a mesh axis runs over, the one named last changes fastest.
Arguments:
- frames_in: bfloat16 [4, 8, 4, 128, 1152], P('rep', 'seq'), may hold values from -6 to 6
- conditioning: float32 [4, 1152], P('rep'), may hold values from -6 to 6
- mod_first: bfloat16 [1152, 6912], P('seq'), may hold values from -0.1875 to 0.1875
- qkv_first: bfloat16 [1152, 3456], P('seq'), may hold values from -0.1875 to 0.1875
- out_first: bfloat16 [1152, 1152], P('seq'), may hold values from -0.75 to 0.75
- up_first: bfloat16 [1152, 4608], P('seq'), may hold values from -0.1875 to 0.1875
- down_first: bfloat16 [4608, 1152], P('seq'), may hold values from -0.09375 to 0.09375
- mod_second: bfloat16 [1152, 6912], P('seq'), may hold values from -0.1875 to 0.1875
- qkv_second: bfloat16 [1152, 3456], P('seq'), may hold values from -0.1875 to 0.1875
- out_second: bfloat16 [1152, 1152], P('seq'), may hold values from -0.375 to 0.375
- up_second: bfloat16 [1152, 4608], P('seq'), may hold values from -0.1875 to 0.1875
- down_second: bfloat16 [4608, 1152], P('seq'), may hold values from -0.09375 to 0.09375
- cotangent: float32 [4, 8, 4, 128, 1152], P('rep', 'seq'), may hold values from -6 to 6
Outputs:
- block_out: float32 [4, 8, 4, 128, 1152], P('rep', 'seq')
- input_grad: float32 [4, 8, 4, 128, 1152], P('rep', 'seq')
- conditioning_grad: float32 [4, 1152], P('rep', 'seq')
- mod_first_grad: float32 [1152, 6912], P('seq')
- qkv_first_grad: float32 [1152, 3456], P('seq')
- out_first_grad: float32 [1152, 1152], P('seq')
- up_first_grad: float32 [1152, 4608], P('seq')
- first_down_gradient: float32 [4608, 1152], P('seq')
- mod_second_grad: float32 [1152, 6912], P('seq')
- qkv_second_grad: float32 [1152, 3456], P('seq')
- out_second_grad: float32 [1152, 1152], P('seq')
- up_second_grad: float32 [1152, 4608], P('seq')
- down_second_grad: float32 [4608, 1152], P('seq')
All inputs are finite; a program needn't handle non-finite values.
Results may differ from a plain program's by a relative error of at most 0.02175.
Values may be sent and summed in bfloat16 or wider, within the bound.
A program may use at most 384 MiB of HBM per device.

v0:
```python
import jax
import jax.numpy as jnp
from jax import lax
from jax.sharding import PartitionSpec as P

HEADS = 16
HEAD_WIDTH = 72
norm_epsilon = 1e-06


def from_partner(block, axis, apart):
    count = lax.axis_size(axis)
    route = []
    for low in range(count):
        high = low | 1 << apart
        if high != low and high < count:
            route += [(low, high), (high, low)]
    return lax.ppermute(block, axis, route)


def shortened(x):
    return jax.tree.map(lambda a: a.astype(jnp.bfloat16) if a.dtype == jnp.float32 else a, x)


def layer_mod(stream, shift_part, scale_part):
    row_mean = jnp.mean(stream, axis=-1, keepdims=True)
    centred = stream - row_mean
    row_var = jnp.mean(centred * centred, axis=-1, keepdims=True)
    return centred * lax.rsqrt(row_var + norm_epsilon) * (1.0 + scale_part) + shift_part


def gelu_tanh(pre_value):
    return jax.nn.gelu(pre_value, approximate=True)


def project(left_operand, right_operand):
    return jnp.einsum(
        "csld,de->csle", left_operand, right_operand, preferred_element_type=jnp.float32
    )


def project_back(incoming, right_operand):
    return jnp.einsum("csle,de->csld", incoming, right_operand, preferred_element_type=jnp.float32)


def mod_parts(modulation):
    return [segment[:, None, None, :] for segment in jnp.split(modulation, 6, axis=-1)]


def modulations(conditioning, mod_one, mod_two):
    row_count = mod_one.shape[0]
    row_start = lax.axis_index("seq") * row_count
    silu_local = lax.dynamic_slice_in_dim(
        jax.nn.silu(conditioning), row_start, row_count, 1
    ).astype(jnp.bfloat16)
    part_one = jnp.dot(silu_local, mod_one, preferred_element_type=jnp.float32)
    part_two = jnp.dot(silu_local, mod_two, preferred_element_type=jnp.float32)
    summed = lax.psum((part_one, part_two), "seq")
    return (summed[0], summed[1], silu_local, row_start)


def gather_layer(qkv_w, out_w, up_w, down_w):
    return (
        lax.all_gather(qkv_w, "seq", axis=0, tiled=True),
        lax.all_gather(out_w, "seq", axis=0, tiled=True),
        lax.all_gather(up_w, "seq", axis=0, tiled=True),
        lax.all_gather(down_w, "seq", axis=0, tiled=True),
    )


def gather_layer_again(qkv_w, out_w, up_w, down_w):
    return (
        lax.all_gather(qkv_w, "seq", axis=0, tiled=True),
        lax.all_gather(out_w, "seq", axis=0, tiled=True),
        lax.all_gather(up_w, "seq", axis=0, tiled=True),
        lax.all_gather(down_w, "seq", axis=0, tiled=True),
    )


def partner_values(stacked):
    return from_partner(stacked, "seq", 0)


def partner_grads(stacked):
    return from_partner(stacked.astype(jnp.bfloat16), "seq", 0).astype(stacked.dtype)


def to_places(stream):
    clip_count, frame_dev, half_places, features = stream.shape
    devices = lax.axis_size("seq")
    place_part = half_places // devices
    exchanged = lax.all_to_all(
        stream.reshape(1, clip_count, frame_dev, devices, place_part, features).astype(
            jnp.bfloat16
        ),
        "seq",
        split_axis=3,
        concat_axis=0,
        tiled=True,
    ).astype(jnp.float32)
    exchanged = exchanged.reshape(devices // 2, 2, clip_count, frame_dev, place_part, features)
    exchanged = jnp.transpose(exchanged, (2, 1, 4, 0, 3, 5))
    return exchanged.reshape(clip_count, 2 * place_part, devices // 2 * frame_dev, features)


def to_frames(stream, frame_dev):
    clip_count, place_count, frame_total, features = stream.shape
    devices = lax.axis_size("seq")
    place_part = place_count // 2
    arranged = stream.reshape(clip_count, 2, place_part, devices // 2, frame_dev, features)
    arranged = jnp.transpose(arranged, (3, 1, 0, 4, 2, 5)).reshape(
        devices, clip_count, frame_dev, 1, place_part, features
    )
    exchanged = lax.all_to_all(
        shortened(arranged), "seq", split_axis=0, concat_axis=3, tiled=True
    ).astype(arranged.dtype)
    return exchanged.reshape(clip_count, frame_dev, devices * place_part, features)


def forward_layer(stream, modulation, weights, spatial):
    qkv_w, out_w, up_w, down_w = weights
    shift_attn, scale_attn, gate_attn, shift_mlp, scale_mlp, gate_mlp = mod_parts(modulation)
    clip_count, seq_count, seq_len, features = stream.shape
    normed = layer_mod(stream, shift_attn, scale_attn).astype(jnp.bfloat16)
    projected = project(normed, qkv_w).astype(jnp.bfloat16)
    queries, keys_all, values_all = jnp.split(projected, 3, axis=-1)
    if spatial:
        remote = partner_values(jnp.stack([keys_all, values_all]))
        keys_all = jnp.concatenate([keys_all, remote[0]], axis=2)
        values_all = jnp.concatenate([values_all, remote[1]], axis=2)
    key_len = keys_all.shape[2]
    queries = queries.reshape(clip_count, seq_count, seq_len, HEADS, HEAD_WIDTH)
    keys_all = keys_all.reshape(clip_count, seq_count, key_len, HEADS, HEAD_WIDTH)
    values_all = values_all.reshape(clip_count, seq_count, key_len, HEADS, HEAD_WIDTH)
    scores = jnp.einsum(
        "cslhe,csmhe->cshlm", queries, keys_all, preferred_element_type=jnp.float32
    ) * HEAD_WIDTH ** (-0.5)
    peak_score = jnp.max(scores, axis=-1, keepdims=True)
    scaled_exp = jnp.exp(scores - peak_score)
    attention = scaled_exp / jnp.sum(scaled_exp, axis=-1, keepdims=True)
    attention_low = attention.astype(jnp.bfloat16)
    attended = jnp.einsum(
        "cshlm,csmhe->cslhe", attention_low, values_all, preferred_element_type=jnp.float32
    )
    attended = attended.astype(jnp.bfloat16).reshape(clip_count, seq_count, seq_len, features)
    branch = project(attended, out_w)
    middle = stream + gate_attn * branch
    normed_mid = layer_mod(middle, shift_mlp, scale_mlp).astype(jnp.bfloat16)
    hidden_pre = project(normed_mid, up_w)
    hidden = gelu_tanh(hidden_pre).astype(jnp.bfloat16)
    mlp_out = project(hidden, down_w)
    result = middle + gate_mlp * mlp_out
    kept_state = (
        normed,
        queries,
        keys_all,
        values_all,
        attention,
        attention_low,
        attended,
        branch,
        middle,
        normed_mid,
        hidden_pre,
        hidden,
        mlp_out,
    )
    return (result, kept_state)


def backward_layer(result_grad, stream, modulation, weights, kept_state, spatial):
    qkv_w, out_w, up_w, down_w = weights
    (
        normed,
        queries,
        keys_all,
        values_all,
        attention,
        attention_low,
        attended,
        branch,
        middle,
        normed_mid,
        hidden_pre,
        hidden,
        mlp_out,
    ) = kept_state
    shift_attn, scale_attn, gate_attn, shift_mlp, scale_mlp, gate_mlp = mod_parts(modulation)
    clip_count, seq_count, seq_len, features = stream.shape
    gate_mlp_grad = jnp.sum(result_grad * mlp_out, axis=(1, 2))
    mlp_grad = (gate_mlp * result_grad).astype(jnp.bfloat16)
    hidden_grad = project_back(mlp_grad, down_w)
    pre_grad = jax.vjp(gelu_tanh, hidden_pre)[1](hidden_grad)[0].astype(jnp.bfloat16)
    normed_mid_grad = project_back(pre_grad, up_w)
    middle_ln_grad, shift_mlp_grad, scale_mlp_grad = jax.vjp(
        layer_mod, middle, shift_mlp, scale_mlp
    )[1](normed_mid_grad)
    middle_grad = result_grad + middle_ln_grad
    gate_attn_grad = jnp.sum(middle_grad * branch, axis=(1, 2))
    branch_grad = (gate_attn * middle_grad).astype(jnp.bfloat16)
    attended_grad = project_back(branch_grad, out_w).astype(jnp.bfloat16)
    attended_grad = attended_grad.reshape(clip_count, seq_count, seq_len, HEADS, HEAD_WIDTH)
    attention_grad = jnp.einsum(
        "cslhe,csmhe->cshlm", attended_grad, values_all, preferred_element_type=jnp.float32
    )
    scores_grad = attention * (
        attention_grad - jnp.sum(attention_grad * attention, axis=-1, keepdims=True)
    )
    scores_grad = scores_grad.astype(jnp.bfloat16)
    inv_root = HEAD_WIDTH ** (-0.5)
    queries_grad = (
        jnp.einsum("cshlm,csmhe->cslhe", scores_grad, keys_all, preferred_element_type=jnp.float32)
        * inv_root
    )
    keys_grad = (
        jnp.einsum("cshlm,cslhe->csmhe", scores_grad, queries, preferred_element_type=jnp.float32)
        * inv_root
    )
    values_grad = jnp.einsum(
        "cshlm,cslhe->csmhe", attention_low, attended_grad, preferred_element_type=jnp.float32
    )
    if spatial:
        returned = partner_grads(
            jnp.stack([keys_grad[:, :, seq_len:], values_grad[:, :, seq_len:]])
        )
        keys_grad = keys_grad[:, :, :seq_len] + returned[0]
        values_grad = values_grad[:, :, :seq_len] + returned[1]
    qkv_grad = jnp.concatenate(
        [
            component.reshape(clip_count, seq_count, seq_len, features)
            for component in (queries_grad, keys_grad, values_grad)
        ],
        axis=-1,
    )
    qkv_grad = qkv_grad.astype(jnp.bfloat16)
    normed_grad = project_back(qkv_grad, qkv_w)
    stream_ln_grad, attention_shift_gradient, scale_attn_grad = jax.vjp(
        layer_mod, stream, shift_attn, scale_attn
    )[1](normed_grad)
    stream_grad = middle_grad + stream_ln_grad
    mod_grad = jnp.concatenate(
        [
            attention_shift_gradient.reshape(clip_count, features),
            scale_attn_grad.reshape(clip_count, features),
            gate_attn_grad,
            shift_mlp_grad.reshape(clip_count, features),
            scale_mlp_grad.reshape(clip_count, features),
            gate_mlp_grad,
        ],
        axis=-1,
    )
    grad_pairs = (
        (normed, qkv_grad),
        (attended, branch_grad),
        (normed_mid, pre_grad),
        (hidden, mlp_grad),
    )
    return (stream_grad, mod_grad, grad_pairs)


def spread_rows_out(left_operand, right_operand):
    left_flat = left_operand.reshape(-1, left_operand.shape[-1])
    right_flat = right_operand.reshape(-1, right_operand.shape[-1])
    return lax.psum_scatter(
        jnp.einsum("nd,ne->de", left_flat, right_flat, preferred_element_type=jnp.float32).astype(
            jnp.bfloat16
        ),
        "seq",
        scatter_dimension=0,
        tiled=True,
    ).astype(jnp.float32)


def layer_grads(grad_pairs):
    return tuple(
        (spread_rows_out(grad_pairs[index][0], grad_pairs[index][1]) for index in range(4))
    )


def per_device(
    frames_in,
    conditioning,
    mod_first,
    qkv_first,
    out_first,
    up_first,
    down_first,
    mod_second,
    qkv_second,
    out_second,
    up_second,
    down_second,
    cotangent,
):
    clip_count = frames_in.shape[0]
    frame_dev = frames_in.shape[2]
    half_places = frames_in.shape[3]
    features = frames_in.shape[4]
    start_stream = frames_in.reshape(clip_count, frame_dev, half_places, features).astype(
        jnp.float32
    )
    mod_one, mod_two, silu_local, row_start = modulations(conditioning, mod_first, mod_second)
    weights_one = gather_layer(qkv_first, out_first, up_first, down_first)
    spatial_out, unused_one = forward_layer(start_stream, mod_one, weights_one, True)
    weights_two = gather_layer(qkv_second, out_second, up_second, down_second)
    temporal_out, unused_two = forward_layer(to_places(spatial_out), mod_two, weights_two, False)
    block_out = to_frames(temporal_out, frame_dev)
    mod_one, mod_two, silu_local, row_start = modulations(conditioning, mod_first, mod_second)
    again_one = gather_layer_again(qkv_first, out_first, up_first, down_first)
    spatial_again, state_one = forward_layer(start_stream, mod_one, again_one, True)
    again_two = gather_layer_again(qkv_second, out_second, up_second, down_second)
    placed_again = to_places(spatial_again)
    unused_three, state_two = forward_layer(placed_again, mod_two, again_two, False)
    cotangent_sites = to_places(cotangent.reshape(clip_count, frame_dev, half_places, features))
    placed_grad, mod_grad_two, pairs_two = backward_layer(
        cotangent_sites, placed_again, mod_two, again_two, state_two, False
    )
    row_attn = qkv_first.shape[0]
    grads_two = layer_grads(pairs_two)
    spatial_grad = to_frames(placed_grad, frame_dev)
    stream_grad, mod_grad_one, pairs_one = backward_layer(
        spatial_grad, start_stream, mod_one, again_one, state_one, True
    )
    grads_one = layer_grads(pairs_one)
    mod_totals = (
        lax.psum(mod_grad_one.astype(jnp.bfloat16), "seq").astype(jnp.float32),
        lax.psum(mod_grad_two.astype(jnp.bfloat16), "seq").astype(jnp.float32),
    )
    low_one = mod_totals[0].astype(jnp.bfloat16)
    low_two = mod_totals[1].astype(jnp.bfloat16)
    mod_weight_one = jnp.einsum(
        "cd,ce->de", silu_local, low_one, preferred_element_type=jnp.float32
    )
    mod_weight_two = jnp.einsum(
        "cd,ce->de", silu_local, low_two, preferred_element_type=jnp.float32
    )
    silu_grad = jnp.einsum("ce,de->cd", low_one, mod_first, preferred_element_type=jnp.float32)
    silu_grad = silu_grad + jnp.einsum(
        "ce,de->cd", low_two, mod_second, preferred_element_type=jnp.float32
    )
    condition_local = lax.dynamic_slice_in_dim(conditioning, row_start, row_attn, 1)
    condition_grad = jax.vjp(jax.nn.silu, condition_local)[1](silu_grad)[0]
    summed = (
        lax.psum(mod_weight_one.astype(jnp.bfloat16), "rep").astype(jnp.float32),
        lax.psum(grads_one[0].astype(jnp.bfloat16), "rep").astype(jnp.float32),
        lax.psum(grads_one[1].astype(jnp.bfloat16), "rep").astype(jnp.float32),
        lax.psum(grads_one[2].astype(jnp.bfloat16), "rep").astype(jnp.float32),
        lax.psum(grads_one[3].astype(jnp.bfloat16), "rep").astype(jnp.float32),
        lax.psum(mod_weight_two.astype(jnp.bfloat16), "rep").astype(jnp.float32),
        lax.psum(grads_two[0].astype(jnp.bfloat16), "rep").astype(jnp.float32),
        lax.psum(grads_two[1].astype(jnp.bfloat16), "rep").astype(jnp.float32),
        lax.psum(grads_two[2].astype(jnp.bfloat16), "rep").astype(jnp.float32),
        lax.psum(grads_two[3].astype(jnp.bfloat16), "rep").astype(jnp.float32),
    )
    out_shape = (clip_count, 1, frame_dev, half_places, features)
    return (
        block_out.reshape(out_shape),
        stream_grad.reshape(out_shape),
        condition_grad,
        summed[0],
        summed[1],
        summed[2],
        summed[3],
        summed[4],
        summed[5],
        summed[6],
        summed[7],
        summed[8],
        summed[9],
    )


def solution(mesh):
    return jax.shard_map(
        per_device,
        mesh=mesh,
        in_specs=(
            P("rep", "seq", None, None, None),
            P("rep", None),
            P("seq", None),
            P("seq", None),
            P("seq", None),
            P("seq", None),
            P("seq", None),
            P("seq", None),
            P("seq", None),
            P("seq", None),
            P("seq", None),
            P("seq", None),
            P("rep", "seq", None, None, None),
        ),
        out_specs=(
            P("rep", "seq", None, None, None),
            P("rep", "seq", None, None, None),
            P("rep", "seq"),
            P("seq", None),
            P("seq", None),
            P("seq", None),
            P("seq", None),
            P("seq", None),
            P("seq", None),
            P("seq", None),
            P("seq", None),
            P("seq", None),
            P("seq", None),
        ),
        check_vma=False,
    )
```

profile of v0, /device:TPU:0, one launch (start us, length us, event | category | flops | bytes accessed | tf_op | source)
XLA Modules:
  0.0 1629.8 jit_solution(10004412810075176240)
XLA Ops:
  17.6 26.8 %all-reduce = (f32[1,6912]{1,0:T(1,128)S(1)}, f32[1,6912]{1,0:T(1,128)S(1)}) all-reduce(f32[1,6912]{1,0:T(1,128)S(1)} %fusion.149, f32[1,6912]{1,0:T(1,128)S(1)} %fusion.147), channel_id=1, replica_groups=mesh['rep'=4,'seq'=8] {'seq'}, use_global_device_ids=true, to_apply=%region_0.1 | all-reduce | flops 13824 | bytes 110592 | tf_op jit(solution)/shard_map/psum | solution.py:58
  44.6 21.0 %all-gather.9.cloned.1.call-done = bf16[1152,3456]{1,0:T(8,128)(2,1)} async-done(((bf16[144,3456]{1,0:T(8,128)(2,1)}), bf16[1152,3456]{1,0:T(8,128)(2,1)}) %all-gather.9.cloned.1.call-update) | async-done | bytes 7962640 | tf_op jit(solution)/shard_map/all_gather | solution.py:64
  109.1 22.1 %fusion.119 = bf16[4,16,72,128]{3,2,1,0:T(8,128)(2,1)} fusion(bf16[1,4,128,16,72]{2,4,3,1,0:T(8,128)(2,1)} %bitcast.356, bf16[1,4,128,16,72]{2,4,3,1,0:T(8,128)(2,1)} %bitcast.354, f32[4,16,128]{2,1,0:T(8,128)S(1)} %get-tuple-element.81, f32[4,16,128,256]{3,2,1,0:T(8,128)} %copy-done.5), kind=kOutput, calls=%fused_computation.180 | convolution fusion | flops 317792512 | bytes 11960320 | tf_op jit(solution)/shard_map/cshlm,csmhe->cslhe/dot_general | solution.py:142
  138.6 36.5 %all-gather.13.cloned.1.call-done = bf16[1152,4608]{1,0:T(8,128)(2,1)} async-done(((bf16[144,4608]{1,0:T(8,128)(2,1)}), bf16[1152,4608]{1,0:T(8,128)(2,1)}) %all-gather.13.cloned.1.call-update) | async-done | bytes 10616848 | tf_op jit(solution)/shard_map/all_gather | solution.py:66
  175.1 23.9 %fusion.22 = f32[4,128,4608]{2,1,0:T(8,128)} fusion(bf16[1152,4608]{1,0:T(8,128)(2,1)} %all-gather.13.cloned.1.call-done, f32[4,128,1152]{2,1,0:T(8,128)} %copy-done.3, f32[1152]{0:T(1024)S(1)} %get-tuple-element.32, f32[1152]{0:T(1024)S(1)} %get-tuple-element.33, f32[4,128]{1,0:T(4,128)S(1)} %fusion.144, f32[4,128]{1,0:T(4,128)S(1)} %broadcast_multiply_fusion.2), kind=kOutput, calls=%fused_computation.32 | convolution fusion | flops 5438767104 | bytes 22426624 | tf_op jit(solution)/shard_map/csld,de->csle/dot_general | solution.py:37
  199.1 41.6 %all-gather.15.cloned.1.call-done = bf16[4608,1152]{1,0:T(8,128)(2,1)} async-done(((bf16[576,1152]{1,0:T(8,128)(2,1)}), bf16[4608,1152]{1,0:T(8,128)(2,1)}) %all-gather.15.cloned.1.call-update) | async-done | bytes 10616848 | tf_op jit(solution)/shard_map/all_gather | solution.py:67
  240.7 13.8 add_convert_fusion.4
  330.9 16.3 %fusion.179 = (f32[32,16,16]{2,1,0:T(8,128)S(1)}, f32[32,16,16,16]{2,3,1,0:T(8,128)S(1)}) fusion(f32[32,16,16,16]{2,3,1,0:T(8,128)S(1)} %fusion.109), kind=kOutput, calls=%fused_computation.279 | output fusion | flops 524303 | bytes 1081344 | tf_op jit(solution)/shard_map/sub | solution.py:139
  363.9 34.0 %all-gather.21.cloned.1.call-done = bf16[1152,4608]{1,0:T(8,128)(2,1)} async-done(((bf16[144,4608]{1,0:T(8,128)(2,1)}), bf16[1152,4608]{1,0:T(8,128)(2,1)}) %all-gather.21.cloned.1.call-update) | async-done | bytes 10616848 | tf_op jit(solution)/shard_map/all_gather | solution.py:66
  397.9 13.2 fusion.14
  411.1 52.6 %all-gather.23.cloned.1.call-done = bf16[4608,1152]{1,0:T(8,128)(2,1)} async-done(((bf16[576,1152]{1,0:T(8,128)(2,1)}), bf16[4608,1152]{1,0:T(8,128)(2,1)}) %all-gather.23.cloned.1.call-update) | async-done | bytes 10616848 | tf_op jit(solution)/shard_map/all_gather | solution.py:67
  463.7 16.0 fusion.37
  479.6 13.5 multiply_reduce_fusion.13
  497.5 18.1 %multiply_reduce_fusion.4 = (bf16[1152]{0:T(1024)(128)(2,1)}, bf16[32,16,1152]{2,1,0:T(8,128)(2,1)}, bf16[1152]{0:T(1024)(128)(2,1)}, f32[32,16,1152]{2,1,0:T(8,128)S(1)}) fusion(f32[32,16,1152]{2,1,0:T(8,128)} %reshape.1279, f32[32,16,1152]{2,1,0:T(8,128)} %get-tuple-element.59, f32[1152]{0:T(1024)S(1)} %get-tuple-element.25, ...), kind=kOutput, calls=%fused_computation.133 | convolution fusion | flops 5465896960 | bytes 33052160 | tf_op jit(solution)/shard_map/csld,de->csle/dot_general | solution.py:37
  563.1 10.9 multiply_reduce_fusion.12
  606.5 17.4 %fusion.30 = bf16[4,128,4608]{2,1,0:T(8,128)(2,1)} fusion(f32[4,128,4608]{2,1,0:T(8,128)} %fusion.22, bf16[4608,1152]{1,0:T(8,128)(2,1)} %all-gather.15.cloned.1.call-done, f32[4,128,1152]{2,1,0:T(8,128)S(1)} %bitcast.337, f32[1152]{0:T(1024)S(1)} %copy-done.64), kind=kOutput, calls=%fused_computation.40 | convolution fusion | flops 5484183552 | bytes 27136512 | tf_op jit(solution)/shard_map/csle,de->csld/dot_general | solution.py:43
  624.0 11.9 multiply_reduce_fusion.11
  646.3 10.6 fusion.7
  664.3 22.2 %convolution_bitcast_fusion.6 = f32[1,4,256,16,72]{2,4,3,1,0:T(8,128)} fusion(bf16[4,128,16,72]{1,3,2,0:T(8,128)(2,1)} %bitcast.360, f32[4,16,128]{2,1,0:T(8,128)S(1)} %copy-done.54, f32[4,16,128,256]{3,2,1,0:T(8,128)} %copy-done.5), kind=kOutput, calls=%fused_computation.161 | convolution fusion | flops 312484096 | bytes 14319616 | tf_op jit(solution)/shard_map/cshlm,cslhe->csmhe/dot_general | solution.py:219
  732.1 13.0 fusion.3
  745.8 11.2 fusion.2
  758.5 12.1 fusion.5
  771.3 11.5 fusion.4
  784.2 10.9 fusion.85
  797.8 23.5 %all-reduce.1 = (bf16[6912]{0:T(1024)(128)(2,1)S(1)}, bf16[6912]{0:T(1024)(128)(2,1)S(1)}) all-reduce(bf16[6912]{0:T(1024)(128)(2,1)S(1)} %reduce.79, bf16[6912]{0:T(1024)(128)(2,1)S(1)} %reduce.80), channel_id=1, replica_groups=mesh['rep'=4,'seq'=8] {'seq'}, use_global_device_ids=true, to_apply=%region_30.31 | all-reduce | flops 13824 | bytes 55296 | tf_op jit(solution)/shard_map/psum | solution.py:326
  823.8 20.3 %reduce-scatter.9.cloned.1.call-done = bf16[144,3456]{1,0:T(8,128)(2,1)} async-done(((bf16[1152,3456]{1,0:T(8,128)(2,1)}), bf16[144,3456]{1,0:T(8,128)(2,1)}) %reduce-scatter.9.cloned.1.call-update) | async-done | bytes 995344 | tf_op jit(solution)/shard_map/reduce_scatter | solution.py:264
  844.1 85.7 %reduce-scatter.23.cloned.1.call-done = bf16[576,1152]{1,0:T(8,128)(2,1)} async-done(((bf16[4608,1152]{1,0:T(8,128)(2,1)}), bf16[576,1152]{1,0:T(8,128)(2,1)}) %reduce-scatter.23.cloned.1.call-update) | async-done | bytes 1327120 | tf_op jit(solution)/shard_map/reduce_scatter | solution.py:264
  929.8 85.6 %reduce-scatter.21.cloned.1.call-done = bf16[144,4608]{1,0:T(8,128)(2,1)} async-done(((bf16[1152,4608]{1,0:T(8,128)(2,1)}), bf16[144,4608]{1,0:T(8,128)(2,1)}) %reduce-scatter.21.cloned.1.call-update) | async-done | bytes 1327120 | tf_op jit(solution)/shard_map/reduce_scatter | solution.py:264
  1015.4 85.6 %reduce-scatter.15.cloned.1.call-done = bf16[576,1152]{1,0:T(8,128)(2,1)} async-done(((bf16[4608,1152]{1,0:T(8,128)(2,1)}), bf16[576,1152]{1,0:T(8,128)(2,1)}) %reduce-scatter.15.cloned.1.call-update) | async-done | bytes 1327120 | tf_op jit(solution)/shard_map/reduce_scatter | solution.py:264
  1101.0 85.6 %reduce-scatter.13.cloned.1.call-done = bf16[144,4608]{1,0:T(8,128)(2,1)} async-done(((bf16[1152,4608]{1,0:T(8,128)(2,1)}), bf16[144,4608]{1,0:T(8,128)(2,1)}) %reduce-scatter.13.cloned.1.call-update) | async-done | bytes 1327120 | tf_op jit(solution)/shard_map/reduce_scatter | solution.py:264
  1191.4 19.3 %all_to_all.16 = bf16[8,1,4,1,16,1152]{5,4,2,3,1,0:T(8,128)(2,1)S(1)} all-to-all(bf16[8,1,4,1,16,1152]{5,4,2,3,1,0:T(8,128)(2,1)S(1)} %bitcast.348), channel_id=1, replica_groups=mesh['rep'=4,'seq'=8] {'seq'}, dimensions={0} | all-to-all | bytes 2359296 | tf_op jit(solution)/shard_map/all_to_all | solution.py:114
  1217.3 386.7 %all-reduce.5.cloned.1.call-done = (bf16[144,6912]{1,0:T(8,128)(2,1)}, bf16[144,3456]{1,0:T(8,128)(2,1)}, bf16[144,1152]{1,0:T(8,128)(2,1)}, bf16[144,4608]{1,0:...) async-done(((bf16[144,6912]{1,0:T(8,128)(2,1)}, ...) | async-done | bytes 11943952 | tf_op jit(solution)/shard_map/psum | solution.py:344
  (435 shorter events, 340.9 us)
Async XLA Ops:
  7.2 58.4 %all-gather.9.cloned.1.call-start = ((), (), s32[]{:S(2)}) async-start(), calls=%async_computation.12 | async-start | bytes 8957952 | tf_op jit(solution)/shard_map/all_gather | solution.py:64
  7.9 123.3 %all-gather.11.cloned.1.call-start = ((), (), s32[]{:S(2)}) async-start(), calls=%async_computation.13 | async-start | bytes 2985984 | tf_op jit(solution)/shard_map/all_gather | solution.py:65
  8.7 166.4 %all-gather.13.cloned.1.call-start = ((), (), s32[]{:S(2)}) async-start(), calls=%async_computation.14 | async-start | bytes 11943936 | tf_op jit(solution)/shard_map/all_gather | solution.py:66
  9.4 231.3 %all-gather.15.cloned.1.call-start = ((), (), s32[]{:S(2)}) async-start(), calls=%async_computation.15 | async-start | bytes 11943936 | tf_op jit(solution)/shard_map/all_gather | solution.py:67
  10.0 290.4 %all-gather.17.cloned.1.call-start = ((), (), s32[]{:S(2)}) async-start(), calls=%async_computation.16 | async-start | bytes 8957952 | tf_op jit(solution)/shard_map/all_gather | solution.py:64
  10.6 344.4 %all-gather.19.cloned.1.call-start = ((), (), s32[]{:S(2)}) async-start(), calls=%async_computation.17 | async-start | bytes 2985984 | tf_op jit(solution)/shard_map/all_gather | solution.py:65
  11.2 386.8 %all-gather.21.cloned.1.call-start = ((), (), s32[]{:S(2)}) async-start(), calls=%async_computation.18 | async-start | bytes 11943936 | tf_op jit(solution)/shard_map/all_gather | solution.py:66
  11.9 451.7 %all-gather.23.cloned.1.call-start = ((), (), s32[]{:S(2)}) async-start(), calls=%async_computation.19 | async-start | bytes 11943936 | tf_op jit(solution)/shard_map/all_gather | solution.py:67
  44.6 86.6 %copy-start.49 = (f32[1152]{0:T(1024)}, f32[1152]{0:T(1024)S(1)}, u32[]{:S(2)}) copy-start(f32[1152]{0:T(1024)S(1)} %get-tuple-element.36) | copy-start | bytes 13828
  44.6 130.5 %copy-start.55 = (f32[1152]{0:T(1024)}, f32[1152]{0:T(1024)S(1)}, u32[]{:S(2)}) copy-start(f32[1152]{0:T(1024)S(1)} %get-tuple-element.33) | copy-start | bytes 13828
  44.6 130.5 %copy-start.94 = (f32[1152]{0:T(1024)}, f32[1152]{0:T(1024)S(1)}, u32[]{:S(2)}) copy-start(f32[1152]{0:T(1024)S(1)} %get-tuple-element.32) | copy-start | bytes 13828
  44.6 196.1 %copy-start.63 = (f32[1152]{0:T(1024)}, f32[1152]{0:T(1024)S(1)}, u32[]{:S(2)}) copy-start(f32[1152]{0:T(1024)S(1)} %get-tuple-element.31) | copy-start | bytes 13828
  78.1 13.9 collective-permute-start
  80.2 175.4 %all-to-all-start.2 = ((bf16[1,1,4,8,16,1152]{5,4,2,1,0,3:T(8,128)(2,1)}), bf16[1,1,4,8,16,1152]{5,4,2,1,0,3:T(8,128)(2,1)}, u32[]{:S(2)}, u32[]{:S(2)}) async-start(bf16[1,1,4,8,16,1152]{5,4,2,1,0,3:T(8,128)(2,1)} %copy.281), calls=%async_computation.2 | async-start | bytes 2359296 | tf_op jit(solution)/shard_map/all_to_all | solution.py:92
  136.8 62.3 %copy-start.73 = (f32[4,128]{1,0:T(4,128)}, f32[4,128]{1,0:T(4,128)S(1)}, u32[]{:S(2)}) copy-start(f32[4,128]{1,0:T(4,128)S(1)} %broadcast_multiply_fusion.2) | copy-start | bytes 6148
  255.6 21.5 %all-to-all-start = ((bf16[1,1,4,8,16,1152]{5,4,2,1,0,3:T(8,128)(2,1)}), bf16[1,1,4,8,16,1152]{5,4,2,1,0,3:T(8,128)(2,1)S(1)}, u32[]{:S(2)}, u32[]{:S(2)}) async-start(bf16[1,1,4,8,16,1152]{5,4,2,1,0,3:T(8,128)(2,1)} %copy.260), calls=%async_computation | async-start | bytes 2359296 | tf_op jit(solution)/shard_map/all_to_all | solution.py:92
  259.3 138.6 %copy-start.98 = (f32[1152]{0:T(1024)}, f32[1152]{0:T(1024)S(1)}, u32[]{:S(2)}) copy-start(f32[1152]{0:T(1024)S(1)} %get-tuple-element.26) | copy-start | bytes 13828
  259.3 238.2 %copy-start.66 = (f32[1152]{0:T(1024)}, f32[1152]{0:T(1024)S(1)}, u32[]{:S(2)}) copy-start(f32[1152]{0:T(1024)S(1)} %get-tuple-element.27) | copy-start | bytes 13828
  259.3 238.2 %copy-start.68 = (f32[1152]{0:T(1024)}, f32[1152]{0:T(1024)S(1)}, u32[]{:S(2)}) copy-start(f32[1152]{0:T(1024)S(1)} %get-tuple-element.25) | copy-start | bytes 13828
  361.7 135.8 %copy-start.51 = (f32[32,16]{1,0:T(8,128)}, f32[32,16]{1,0:T(8,128)S(1)}, u32[]{:S(2)}) copy-start(f32[32,16]{1,0:T(8,128)S(1)} %copy.275) | copy-start | bytes 6148
  363.9 133.6 %copy-start.61 = (f32[32,16]{1,0:T(8,128)}, f32[32,16]{1,0:T(8,128)S(1)}, u32[]{:S(2)}) copy-start(f32[32,16]{1,0:T(8,128)S(1)} %copy.277) | copy-start | bytes 6148
  586.0 20.3 %all-to-all-start.3 = ((bf16[8,1,4,1,16,1152]{5,4,2,3,1,0:T(8,128)(2,1)}), bf16[8,1,4,1,16,1152]{5,4,2,3,1,0:T(8,128)(2,1)S(1)}, u32[]{:S(2)}, u32[]{:S(2)}) async-start(bf16[8,1,4,1,16,1152]{5,4,2,3,1,0:T(8,128)(2,1)} %bitcast.346), calls=%async_computation.3 | async-start | bytes 2359296 | tf_op jit(solution)/shard_map/all_to_all | solution.py:114
  589.5 234.3 %reduce-scatter.19.cloned.1.call-start = ((), (), s32[]{:S(2)}) async-start(), calls=%async_computation.25 | async-start | bytes 2985984 | tf_op jit(solution)/shard_map/reduce_scatter | solution.py:264
  602.3 221.5 %reduce-scatter.11.cloned.1.call-start = ((), (), s32[]{:S(2)}) async-start(), calls=%async_computation.21 | async-start | bytes 2985984 | tf_op jit(solution)/shard_map/reduce_scatter | solution.py:264
  645.7 178.1 %reduce-scatter.17.cloned.1.call-start = ((), (), s32[]{:S(2)}) async-start(), calls=%async_computation.24 | async-start | bytes 8957952 | tf_op jit(solution)/shard_map/reduce_scatter | solution.py:264
  657.0 187.1 %reduce-scatter.9.cloned.1.call-start = ((), (), s32[]{:S(2)}) async-start(), calls=%async_computation.20 | async-start | bytes 8957952 | tf_op jit(solution)/shard_map/reduce_scatter | solution.py:264
  703.0 5.3 collective-permute-start.1
  730.9 199.0 %reduce-scatter.23.cloned.1.call-start = ((), (), s32[]{:S(2)}) async-start(), calls=%async_computation.27 | async-start | bytes 11943936 | tf_op jit(solution)/shard_map/reduce_scatter | solution.py:264
  745.1 270.3 %reduce-scatter.21.cloned.1.call-start = ((), (), s32[]{:S(2)}) async-start(), calls=%async_computation.26 | async-start | bytes 11943936 | tf_op jit(solution)/shard_map/reduce_scatter | solution.py:264
  757.0 344.0 %reduce-scatter.15.cloned.1.call-start = ((), (), s32[]{:S(2)}) async-start(), calls=%async_computation.23 | async-start | bytes 11943936 | tf_op jit(solution)/shard_map/reduce_scatter | solution.py:264
  770.6 416.0 %reduce-scatter.13.cloned.1.call-start = ((), (), s32[]{:S(2)}) async-start(), calls=%async_computation.22 | async-start | bytes 11943936 | tf_op jit(solution)/shard_map/reduce_scatter | solution.py:264
  782.9 821.1 %all-reduce.5.cloned.1.call-start = ((), (), s32[]{:S(2)}) async-start(), calls=%async_computation.28 | async-start | bytes 23887872 | tf_op jit(solution)/shard_map/psum | solution.py:344
  (99 other events, 746.2 us)
Sparse Core Ops, SparseCore 0:
  9.9 55.5 all-gather.8
  67.4 38.6 all-gather.10
  108.1 66.9 all-gather.12
  176.8 63.8 all-gather.14
  242.4 57.9 all-gather.16
  302.2 29.9 all-gather.18
  334.1 63.8 all-gather.20
  399.8 63.8 all-gather.22
  602.4 45.0 reduce-scatter.18
  651.8 43.7 reduce-scatter.10
  699.2 70.5 reduce-scatter.16
  773.5 70.5 reduce-scatter.8
  847.6 82.1 reduce-scatter.22
  933.2 82.2 reduce-scatter.20
  1018.8 82.2 reduce-scatter.14
  1104.4 82.2 reduce-scatter.12
  1191.6 412.4 all-reduce.4
where the time goes:
time: 1640 us; the launch traced here: 1630 us
  waiting for transfers between devices  963 us (59%)
  matrix products  338 us (21%)
  local copies, waits for them, and re-layouts  141 us (9%)
  other arithmetic  90 us (5%)
  blocking collectives  69.6 us (4%)
    psum x1, waiting for transfers between devices, per_device(): lax.psum(mod_weight_one.astype(jnp.bfloat16), 'rep').astype(jnp.float32)  387 us
    reduce_scatter x8, waiting for transfers between devices, spread_rows_out(): lax.psum_scatter(jnp.einsum('nd,ne->de', left_flat, right_flat, preferred...  363 us
    dot_general x8, matrix products, project(): jnp.einsum('csld,de->csle', left_operand, right_operand, preferred_elemen...  99 us
    all_gather x2, waiting for transfers between devices, gather_layer(): lax.all_gather(down_w, 'seq', axis=0, tiled=True)  94.2 us
    dot_general x8, matrix products, project_back(): jnp.einsum('csle,de->csld', incoming, right_operand, preferred_element_ty...  87.1 us
    dot_general x8, matrix products, spread_rows_out(): jnp.einsum('nd,ne->de', left_flat, right_flat, preferred_element_type=jnp...  76.2 us
    all_gather x2, waiting for transfers between devices, gather_layer(): lax.all_gather(up_w, 'seq', axis=0, tiled=True)  70.6 us
  transfers between devices with their start and end apart: 22, of which 14 were waited for; matrix products, arithmetic and copies ran while one was open for 25% of the time, Pallas kernels for 0%

commit v1 on v0

--- a/solution.py
+++ b/solution.py
@@ -341,7 +341,9 @@
     condition_local = lax.dynamic_slice_in_dim(conditioning, row_start, row_attn, 1)
     condition_grad = jax.vjp(jax.nn.silu, condition_local)[1](silu_grad)[0]
     summed = (
-        lax.psum(mod_weight_one.astype(jnp.bfloat16), "rep").astype(jnp.float32),
+        jnp.sum(lax.all_gather(mod_weight_one.astype(jnp.bfloat16), "rep"), axis=0).astype(
+            jnp.float32
+        ),
         lax.psum(grads_one[0].astype(jnp.bfloat16), "rep").astype(jnp.float32),
         lax.psum(grads_one[1].astype(jnp.bfloat16), "rep").astype(jnp.float32),
         lax.psum(grads_one[2].astype(jnp.bfloat16), "rep").astype(jnp.float32),

time: 1640 us -> 1710 us (1.043)
  waiting for transfers between devices: 963 us -> 1030 us
    all_gather x0 -> x1, waiting for transfers between devices: none -> 114 us  [per_device(): lax.all_gather(mod_weight_one.astype(jnp.bfloat16), 'rep')]
    psum x1, waiting for transfers between devices: 387 us -> 339 us  [per_device(): lax.psum(grads_one[0].astype(jnp.bfloat16), 'rep').astype(jnp.float32)]
  transfers between devices with their start and end apart: 22 -> 23, of which waited for: 14 -> 15; matrix products, arithmetic and copies ran while one was open for 25% -> 25% of each run, Pallas kernels for 0% -> 0%
where the time goes in v1:
time: 1710 us; the launch traced here: 1700 us
  waiting for transfers between devices  1030 us (60%)
  matrix products  338 us (20%)
  local copies, waits for them, and re-layouts  141 us (8%)
  other arithmetic  97.8 us (6%)
  blocking collectives  69.4 us (4%)
    reduce_scatter x8, waiting for transfers between devices, spread_rows_out(): lax.psum_scatter(jnp.einsum('nd,ne->de', left_flat, right_flat, preferred...  363 us
    psum x1, waiting for transfers between devices, per_device(): lax.psum(grads_one[0].astype(jnp.bfloat16), 'rep').astype(jnp.float32)  339 us
    all_gather x1, waiting for transfers between devices, per_device(): lax.all_gather(mod_weight_one.astype(jnp.bfloat16), 'rep')  114 us
    dot_general x8, matrix products, project(): jnp.einsum('csld,de->csle', left_operand, right_operand, preferred_elemen...  98.9 us
    all_gather x2, waiting for transfers between devices, gather_layer(): lax.all_gather(down_w, 'seq', axis=0, tiled=True)  94.3 us
    dot_general x8, matrix products, project_back(): jnp.einsum('csle,de->csld', incoming, right_operand, preferred_element_ty...  87.1 us
    dot_general x8, matrix products, spread_rows_out(): jnp.einsum('nd,ne->de', left_flat, right_flat, preferred_element_type=jnp...  76.1 us
    all_gather x2, waiting for transfers between devices, gather_layer(): lax.all_gather(up_w, 'seq', axis=0, tiled=True)  70.7 us
  transfers between devices with their start and end apart: 23, of which 15 were waited for; matrix products, arithmetic and copies ran while one was open for 25% of the time, Pallas kernels for 0%

profile of v1, /device:TPU:0, one launch (start us, length us, event | category | flops | bytes accessed | tf_op | source)
XLA Modules:
  0.0 1704.5 jit_solution(6959654916004957153)
XLA Ops:
  17.6 26.8 %all-reduce = (f32[1,6912]{1,0:T(1,128)S(1)}, f32[1,6912]{1,0:T(1,128)S(1)}) all-reduce(f32[1,6912]{1,0:T(1,128)S(1)} %fusion.149, f32[1,6912]{1,0:T(1,128)S(1)} %fusion.147), channel_id=1, replica_groups=mesh['rep'=4,'seq'=8] {'seq'}, use_global_device_ids=true, to_apply=%region_0.1 | all-reduce | flops 13824 | bytes 110592 | tf_op jit(solution)/shard_map/psum | solution.py:58
  44.6 21.0 %all-gather.11.cloned.1.call-done = bf16[1152,3456]{1,0:T(8,128)(2,1)} async-done(((bf16[144,3456]{1,0:T(8,128)(2,1)}), bf16[1152,3456]{1,0:T(8,128)(2,1)}) %all-gather.11.cloned.1.call-update) | async-done | bytes 7962640 | tf_op jit(solution)/shard_map/all_gather | solution.py:64
  109.1 22.0 %fusion.119 = bf16[4,16,72,128]{3,2,1,0:T(8,128)(2,1)} fusion(bf16[1,4,128,16,72]{2,4,3,1,0:T(8,128)(2,1)} %bitcast.358, bf16[1,4,128,16,72]{2,4,3,1,0:T(8,128)(2,1)} %bitcast.356, f32[4,16,128]{2,1,0:T(8,128)S(1)} %get-tuple-element.80, f32[4,16,128,256]{3,2,1,0:T(8,128)} %copy-done.5), kind=kOutput, calls=%fused_computation.180 | convolution fusion | flops 317792512 | bytes 11960320 | tf_op jit(solution)/shard_map/cshlm,csmhe->cslhe/dot_general | solution.py:142
  138.5 36.6 %all-gather.15.cloned.1.call-done = bf16[1152,4608]{1,0:T(8,128)(2,1)} async-done(((bf16[144,4608]{1,0:T(8,128)(2,1)}), bf16[1152,4608]{1,0:T(8,128)(2,1)}) %all-gather.15.cloned.1.call-update) | async-done | bytes 10616848 | tf_op jit(solution)/shard_map/all_gather | solution.py:66
  175.1 23.9 %fusion.22 = f32[4,128,4608]{2,1,0:T(8,128)} fusion(bf16[1152,4608]{1,0:T(8,128)(2,1)} %all-gather.15.cloned.1.call-done, f32[4,128,1152]{2,1,0:T(8,128)} %copy-done.3, f32[1152]{0:T(1024)S(1)} %get-tuple-element.32, f32[1152]{0:T(1024)S(1)} %get-tuple-element.33, f32[4,128]{1,0:T(4,128)S(1)} %fusion.144, f32[4,128]{1,0:T(4,128)S(1)} %broadcast_multiply_fusion.2), kind=kOutput, calls=%fused_computation.32 | convolution fusion | flops 5438767104 | bytes 22426624 | tf_op jit(solution)/shard_map/csld,de->csle/dot_general | solution.py:37
  199.0 41.7 %all-gather.17.cloned.1.call-done = bf16[4608,1152]{1,0:T(8,128)(2,1)} async-done(((bf16[576,1152]{1,0:T(8,128)(2,1)}), bf16[4608,1152]{1,0:T(8,128)(2,1)}) %all-gather.17.cloned.1.call-update) | async-done | bytes 10616848 | tf_op jit(solution)/shard_map/all_gather | solution.py:67
  240.7 13.8 add_convert_fusion.4
  330.9 16.3 fusion.179
  363.8 34.1 %all-gather.23.cloned.1.call-done = bf16[1152,4608]{1,0:T(8,128)(2,1)} async-done(((bf16[144,4608]{1,0:T(8,128)(2,1)}), bf16[1152,4608]{1,0:T(8,128)(2,1)}) %all-gather.23.cloned.1.call-update) | async-done | bytes 10616848 | tf_op jit(solution)/shard_map/all_gather | solution.py:66
  397.9 13.2 fusion.14
  411.1 52.6 %all-gather.25.cloned.1.call-done = bf16[4608,1152]{1,0:T(8,128)(2,1)} async-done(((bf16[576,1152]{1,0:T(8,128)(2,1)}), bf16[4608,1152]{1,0:T(8,128)(2,1)}) %all-gather.25.cloned.1.call-update) | async-done | bytes 10616848 | tf_op jit(solution)/shard_map/all_gather | solution.py:67
  463.7 15.9 fusion.37
  479.6 13.5 multiply_reduce_fusion.13
  497.5 18.1 %multiply_reduce_fusion.4 = (bf16[1152]{0:T(1024)(128)(2,1)}, bf16[32,16,1152]{2,1,0:T(8,128)(2,1)}, bf16[1152]{0:T(1024)(128)(2,1)}, f32[32,16,1152]{2,1,0:T(8,128)S(1)}) fusion(f32[32,16,1152]{2,1,0:T(8,128)} %reshape.1279, f32[32,16,1152]{2,1,0:T(8,128)} %get-tuple-element.58, f32[1152]{0:T(1024)S(1)} %get-tuple-element.25, ...), kind=kOutput, calls=%fused_computation.133 | convolution fusion | flops 5465896960 | bytes 33052160 | tf_op jit(solution)/shard_map/csld,de->csle/dot_general | solution.py:37
  563.1 10.9 multiply_reduce_fusion.12
  606.5 17.4 %fusion.30 = bf16[4,128,4608]{2,1,0:T(8,128)(2,1)} fusion(f32[4,128,4608]{2,1,0:T(8,128)} %fusion.22, bf16[4608,1152]{1,0:T(8,128)(2,1)} %all-gather.17.cloned.1.call-done, f32[4,128,1152]{2,1,0:T(8,128)S(1)} %bitcast.338, f32[1152]{0:T(1024)S(1)} %copy-done.63), kind=kOutput, calls=%fused_computation.40 | convolution fusion | flops 5484183552 | bytes 27136512 | tf_op jit(solution)/shard_map/csle,de->csld/dot_general | solution.py:43
  623.9 11.9 multiply_reduce_fusion.11
  664.3 22.3 %convolution_bitcast_fusion.6 = f32[1,4,256,16,72]{2,4,3,1,0:T(8,128)} fusion(bf16[4,128,16,72]{1,3,2,0:T(8,128)(2,1)} %bitcast.362, f32[4,16,128]{2,1,0:T(8,128)S(1)} %copy-done.53, f32[4,16,128,256]{3,2,1,0:T(8,128)} %copy-done.5), kind=kOutput, calls=%fused_computation.161 | convolution fusion | flops 312484096 | bytes 14319616 | tf_op jit(solution)/shard_map/cshlm,cslhe->csmhe/dot_general | solution.py:219
  732.1 12.9 fusion.3
  745.8 11.1 fusion.2
  758.3 12.1 fusion.5
  771.2 11.5 fusion.4
  784.0 10.9 fusion.85
  797.7 23.3 %all-reduce.1 = (bf16[6912]{0:T(1024)(128)(2,1)S(1)}, bf16[6912]{0:T(1024)(128)(2,1)S(1)}) all-reduce(bf16[6912]{0:T(1024)(128)(2,1)S(1)} %reduce.80, bf16[6912]{0:T(1024)(128)(2,1)S(1)} %reduce.81), channel_id=1, replica_groups=mesh['rep'=4,'seq'=8] {'seq'}, use_global_device_ids=true, to_apply=%region_30.31 | all-reduce | flops 13824 | bytes 55296 | tf_op jit(solution)/shard_map/psum | solution.py:326
  823.8 20.2 %reduce-scatter.9.cloned.1.call-done = bf16[144,3456]{1,0:T(8,128)(2,1)} async-done(((bf16[1152,3456]{1,0:T(8,128)(2,1)}), bf16[144,3456]{1,0:T(8,128)(2,1)}) %reduce-scatter.9.cloned.1.call-update) | async-done | bytes 995344 | tf_op jit(solution)/shard_map/reduce_scatter | solution.py:264
  844.0 85.8 %reduce-scatter.23.cloned.1.call-done = bf16[576,1152]{1,0:T(8,128)(2,1)} async-done(((bf16[4608,1152]{1,0:T(8,128)(2,1)}), bf16[576,1152]{1,0:T(8,128)(2,1)}) %reduce-scatter.23.cloned.1.call-update) | async-done | bytes 1327120 | tf_op jit(solution)/shard_map/reduce_scatter | solution.py:264
  929.8 85.6 %reduce-scatter.21.cloned.1.call-done = bf16[144,4608]{1,0:T(8,128)(2,1)} async-done(((bf16[1152,4608]{1,0:T(8,128)(2,1)}), bf16[144,4608]{1,0:T(8,128)(2,1)}) %reduce-scatter.21.cloned.1.call-update) | async-done | bytes 1327120 | tf_op jit(solution)/shard_map/reduce_scatter | solution.py:264
  1015.4 85.6 %reduce-scatter.15.cloned.1.call-done = bf16[576,1152]{1,0:T(8,128)(2,1)} async-done(((bf16[4608,1152]{1,0:T(8,128)(2,1)}), bf16[576,1152]{1,0:T(8,128)(2,1)}) %reduce-scatter.15.cloned.1.call-update) | async-done | bytes 1327120 | tf_op jit(solution)/shard_map/reduce_scatter | solution.py:264
  1101.0 85.6 %reduce-scatter.13.cloned.1.call-done = bf16[144,4608]{1,0:T(8,128)(2,1)} async-done(((bf16[1152,4608]{1,0:T(8,128)(2,1)}), bf16[144,4608]{1,0:T(8,128)(2,1)}) %reduce-scatter.13.cloned.1.call-update) | async-done | bytes 1327120 | tf_op jit(solution)/shard_map/reduce_scatter | solution.py:264
  1191.3 19.3 %all_to_all.16 = bf16[8,1,4,1,16,1152]{5,4,2,3,1,0:T(8,128)(2,1)S(1)} all-to-all(bf16[8,1,4,1,16,1152]{5,4,2,3,1,0:T(8,128)(2,1)S(1)} %bitcast.350), channel_id=1, replica_groups=mesh['rep'=4,'seq'=8] {'seq'}, dimensions={0} | all-to-all | bytes 2359296 | tf_op jit(solution)/shard_map/all_to_all | solution.py:114
  1217.2 114.1 %all-gather.27.cloned.1.call-done = bf16[576,6912]{1,0:T(8,128)(2,1)} async-done(((bf16[144,6912]{1,0:T(8,128)(2,1)}), bf16[576,6912]{1,0:T(8,128)(2,1)}) %all-gather.27.cloned.1.call-update) | async-done | bytes 7962640 | tf_op jit(solution)/shard_map/all_gather | solution.py:344
  1341.3 339.4 %all-reduce.5.cloned.1.call-done = (bf16[144,3456]{1,0:T(8,128)(2,1)}, bf16[144,1152]{1,0:T(8,128)(2,1)}, bf16[144,4608]{1,0:T(8,128)(2,1)}, bf16[576,1152]{1,0:...) async-done(((bf16[144,3456]{1,0:T(8,128)(2,1)}, ...) | async-done | bytes 9953296 | tf_op jit(solution)/shard_map/psum | solution.py:347
  (437 shorter events, 359.5 us)
Async XLA Ops:
  7.2 58.4 %all-gather.11.cloned.1.call-start = ((), (), s32[]{:S(2)}) async-start(), calls=%async_computation.12 | async-start | bytes 8957952 | tf_op jit(solution)/shard_map/all_gather | solution.py:64
  7.9 123.2 %all-gather.13.cloned.1.call-start = ((), (), s32[]{:S(2)}) async-start(), calls=%async_computation.13 | async-start | bytes 2985984 | tf_op jit(solution)/shard_map/all_gather | solution.py:65
  8.7 166.4 %all-gather.15.cloned.1.call-start = ((), (), s32[]{:S(2)}) async-start(), calls=%async_computation.14 | async-start | bytes 11943936 | tf_op jit(solution)/shard_map/all_gather | solution.py:66
  9.4 231.2 %all-gather.17.cloned.1.call-start = ((), (), s32[]{:S(2)}) async-start(), calls=%async_computation.15 | async-start | bytes 11943936 | tf_op jit(solution)/shard_map/all_gather | solution.py:67
  10.0 290.4 %all-gather.19.cloned.1.call-start = ((), (), s32[]{:S(2)}) async-start(), calls=%async_computation.16 | async-start | bytes 8957952 | tf_op jit(solution)/shard_map/all_gather | solution.py:64
  10.6 344.3 %all-gather.21.cloned.1.call-start = ((), (), s32[]{:S(2)}) async-start(), calls=%async_computation.17 | async-start | bytes 2985984 | tf_op jit(solution)/shard_map/all_gather | solution.py:65
  11.2 386.8 %all-gather.23.cloned.1.call-start = ((), (), s32[]{:S(2)}) async-start(), calls=%async_computation.18 | async-start | bytes 11943936 | tf_op jit(solution)/shard_map/all_gather | solution.py:66
  11.9 451.7 %all-gather.25.cloned.1.call-start = ((), (), s32[]{:S(2)}) async-start(), calls=%async_computation.19 | async-start | bytes 11943936 | tf_op jit(solution)/shard_map/all_gather | solution.py:67
  44.6 86.6 %copy-start.48 = (f32[1152]{0:T(1024)}, f32[1152]{0:T(1024)S(1)}, u32[]{:S(2)}) copy-start(f32[1152]{0:T(1024)S(1)} %get-tuple-element.36) | copy-start | bytes 13828
  44.6 130.5 %copy-start.54 = (f32[1152]{0:T(1024)}, f32[1152]{0:T(1024)S(1)}, u32[]{:S(2)}) copy-start(f32[1152]{0:T(1024)S(1)} %get-tuple-element.33) | copy-start | bytes 13828
  44.6 130.5 %copy-start.93 = (f32[1152]{0:T(1024)}, f32[1152]{0:T(1024)S(1)}, u32[]{:S(2)}) copy-start(f32[1152]{0:T(1024)S(1)} %get-tuple-element.32) | copy-start | bytes 13828
  44.6 196.1 %copy-start.62 = (f32[1152]{0:T(1024)}, f32[1152]{0:T(1024)S(1)}, u32[]{:S(2)}) copy-start(f32[1152]{0:T(1024)S(1)} %get-tuple-element.31) | copy-start | bytes 13828
  78.1 14.0 collective-permute-start
  80.2 175.4 %all-to-all-start.2 = ((bf16[1,1,4,8,16,1152]{5,4,2,1,0,3:T(8,128)(2,1)}), bf16[1,1,4,8,16,1152]{5,4,2,1,0,3:T(8,128)(2,1)}, u32[]{:S(2)}, u32[]{:S(2)}) async-start(bf16[1,1,4,8,16,1152]{5,4,2,1,0,3:T(8,128)(2,1)} %copy.281), calls=%async_computation.2 | async-start | bytes 2359296 | tf_op jit(solution)/shard_map/all_to_all | solution.py:92
  255.6 21.5 %all-to-all-start = ((bf16[1,1,4,8,16,1152]{5,4,2,1,0,3:T(8,128)(2,1)}), bf16[1,1,4,8,16,1152]{5,4,2,1,0,3:T(8,128)(2,1)S(1)}, u32[]{:S(2)}, u32[]{:S(2)}) async-start(bf16[1,1,4,8,16,1152]{5,4,2,1,0,3:T(8,128)(2,1)} %copy.260), calls=%async_computation | async-start | bytes 2359296 | tf_op jit(solution)/shard_map/all_to_all | solution.py:92
  259.3 138.6 %copy-start.97 = (f32[1152]{0:T(1024)}, f32[1152]{0:T(1024)S(1)}, u32[]{:S(2)}) copy-start(f32[1152]{0:T(1024)S(1)} %get-tuple-element.26) | copy-start | bytes 13828
  259.3 238.2 %copy-start.65 = (f32[1152]{0:T(1024)}, f32[1152]{0:T(1024)S(1)}, u32[]{:S(2)}) copy-start(f32[1152]{0:T(1024)S(1)} %get-tuple-element.27) | copy-start | bytes 13828
  259.3 238.1 %copy-start.67 = (f32[1152]{0:T(1024)}, f32[1152]{0:T(1024)S(1)}, u32[]{:S(2)}) copy-start(f32[1152]{0:T(1024)S(1)} %get-tuple-element.25) | copy-start | bytes 13828
  361.6 135.8 %copy-start.50 = (f32[32,16]{1,0:T(8,128)}, f32[32,16]{1,0:T(8,128)S(1)}, u32[]{:S(2)}) copy-start(f32[32,16]{1,0:T(8,128)S(1)} %copy.275) | copy-start | bytes 6148
  363.8 133.6 %copy-start.60 = (f32[32,16]{1,0:T(8,128)}, f32[32,16]{1,0:T(8,128)S(1)}, u32[]{:S(2)}) copy-start(f32[32,16]{1,0:T(8,128)S(1)} %copy.277) | copy-start | bytes 6148
  586.0 20.3 %all-to-all-start.3 = ((bf16[8,1,4,1,16,1152]{5,4,2,3,1,0:T(8,128)(2,1)}), bf16[8,1,4,1,16,1152]{5,4,2,3,1,0:T(8,128)(2,1)S(1)}, u32[]{:S(2)}, u32[]{:S(2)}) async-start(bf16[8,1,4,1,16,1152]{5,4,2,3,1,0:T(8,128)(2,1)} %bitcast.348), calls=%async_computation.3 | async-start | bytes 2359296 | tf_op jit(solution)/shard_map/all_to_all | solution.py:114
  589.5 234.2 %reduce-scatter.19.cloned.1.call-start = ((), (), s32[]{:S(2)}) async-start(), calls=%async_computation.25 | async-start | bytes 2985984 | tf_op jit(solution)/shard_map/reduce_scatter | solution.py:264
  602.3 221.5 %reduce-scatter.11.cloned.1.call-start = ((), (), s32[]{:S(2)}) async-start(), calls=%async_computation.21 | async-start | bytes 2985984 | tf_op jit(solution)/shard_map/reduce_scatter | solution.py:264
  645.6 178.2 %reduce-scatter.17.cloned.1.call-start = ((), (), s32[]{:S(2)}) async-start(), calls=%async_computation.24 | async-start | bytes 8957952 | tf_op jit(solution)/shard_map/reduce_scatter | solution.py:264
  656.9 187.1 %reduce-scatter.9.cloned.1.call-start = ((), (), s32[]{:S(2)}) async-start(), calls=%async_computation.20 | async-start | bytes 8957952 | tf_op jit(solution)/shard_map/reduce_scatter | solution.py:264
  703.0 5.3 collective-permute-start.1
  730.8 198.9 %reduce-scatter.23.cloned.1.call-start = ((), (), s32[]{:S(2)}) async-start(), calls=%async_computation.27 | async-start | bytes 11943936 | tf_op jit(solution)/shard_map/reduce_scatter | solution.py:264
  745.1 270.3 %reduce-scatter.21.cloned.1.call-start = ((), (), s32[]{:S(2)}) async-start(), calls=%async_computation.26 | async-start | bytes 11943936 | tf_op jit(solution)/shard_map/reduce_scatter | solution.py:264
  756.9 344.1 %reduce-scatter.15.cloned.1.call-start = ((), (), s32[]{:S(2)}) async-start(), calls=%async_computation.23 | async-start | bytes 11943936 | tf_op jit(solution)/shard_map/reduce_scatter | solution.py:264
  770.5 416.1 %reduce-scatter.13.cloned.1.call-start = ((), (), s32[]{:S(2)}) async-start(), calls=%async_computation.22 | async-start | bytes 11943936 | tf_op jit(solution)/shard_map/reduce_scatter | solution.py:264
  782.7 548.5 %all-gather.27.cloned.1.call-start = ((), (), s32[]{:S(2)}) async-start(), calls=%async_computation.28 | async-start | bytes 9953280 | tf_op jit(solution)/shard_map/all_gather | solution.py:344
  823.5 857.3 %all-reduce.5.cloned.1.call-start = ((), (), s32[]{:S(2)}) async-start(), calls=%async_computation.29 | async-start | bytes 19906560 | tf_op jit(solution)/shard_map/psum | solution.py:347
  (99 other events, 809.5 us)
Sparse Core Ops, SparseCore 0:
  9.9 55.5 all-gather.10
  67.4 38.6 all-gather.12
  108.1 66.9 all-gather.14
  176.8 63.8 all-gather.16
  242.4 57.9 all-gather.18
  302.2 29.9 all-gather.20
  334.1 63.8 all-gather.22
  399.8 63.8 all-gather.24
  602.4 45.1 reduce-scatter.18
  651.9 43.7 reduce-scatter.10
  699.2 70.3 reduce-scatter.16
  773.5 70.5 reduce-scatter.8
  847.5 82.1 reduce-scatter.22
  933.1 82.2 reduce-scatter.20
  1018.7 82.1 reduce-scatter.14
  1104.3 82.2 reduce-scatter.12
  1188.6 142.6 all-gather.26
  1335.4 345.2 all-reduce.4
